TPU v7x, 32 devices: a whole 2x2x4 slice. The times are simulated.
32 devices in a mesh: row: 4 (over y, x), col: 8 (over z, core).
Axes of the slice: x: 2, y: 2, z: 4, core: 2. Of those that a mesh axis runs over, the one named last changes fastest.
Arguments:
- iterates: float32 [11, 1024], P(None, ('col', 'row')), may hold values from -6 to 6
- residuals: float32 [11, 1024], P(None, ('col', 'row')), may hold values from -3 to 3
- operator: float32 [16384, 1024], P('row', 'col'), may hold values from -0.1875 to 0.1875
- target: float32 [16384], replicated, may hold values from -6 to 6
- cone_id: int32 [16384], replicated, may hold values from 0 to 2047, never falling along the last dimension, each value on 1 to 16 neighbouring positions
Outputs:
- next_point: float32 [1024], P(('col', 'row'))
- projected: float32 [16384], P('row')
Inputs may be any that keep to these rules, and one draw needn't show every extreme that they name: cone_id never falls along the rows; each of the 2048 cones holds 1 to 16 consecutive rows.
All inputs are finite; a program needn't handle non-finite values.
Results may differ from a plain program's by a relative error of at most 0.0003.
Values sent between devices are 32-bit elements; how exact they have to be, the bound alone decides.
No kernel may reach another device: no remote copies, remote signals or barrier semaphores. Data moves between devices by JAX's collectives and lax.ppermute only.
A program may use at most 64 MiB of HBM per device.

v0:
```python
import math
import jax
import jax.numpy as jnp
from jax import lax
from jax.sharding import PartitionSpec as P

HIGH = lax.Precision.HIGHEST
RIM = 16


def with_halo(x, sides, width):
    for axis, dim in sides:
        devices, length = (lax.axis_size(axis), x.shape[dim])
        up = [(i, (i + 1) % devices) for i in range(devices - 1)]
        down = [(j, i) for i, j in up]
        last = lax.slice_in_dim(x, length - width, length, axis=dim)
        leading = lax.slice_in_dim(x, 0, width, axis=dim)
        before = lax.ppermute(last, axis, up)
        after = lax.ppermute(leading, axis, down)
        x = jnp.concatenate([before, x, after], axis=dim)
    return x


def solve_weights(gram, right_side):
    count = gram.shape[0]
    shifted = gram + 0.01 * (jnp.trace(gram) / count) * jnp.eye(count, dtype=jnp.float32)
    factor = jnp.linalg.cholesky(shifted)
    return jax.scipy.linalg.cho_solve((factor, True), right_side)


def window_cones(slack_ext, ids_ext, head_ext, length):
    shifts = range(1 - RIM, RIM)
    slack_win = jnp.stack([slack_ext[RIM + s : RIM + s + length] for s in shifts])
    ids_win = jnp.stack([ids_ext[RIM + s : RIM + s + length] for s in shifts])
    head_win = jnp.stack([head_ext[RIM + s : RIM + s + length] for s in shifts])
    own_ids = ids_ext[RIM : RIM + length]
    slack = slack_ext[RIM : RIM + length]
    head_own = head_ext[RIM : RIM + length]
    same = (ids_win == own_ids[None, :]).astype(jnp.float32)
    head_row = jnp.sum(same * head_win * slack_win, axis=0)
    tail_tot = jnp.sum(same * (1.0 - head_win) * slack_win * slack_win, axis=0)
    norm_row = jnp.sqrt(tail_tot)
    inside = norm_row <= head_row
    killed = norm_row <= -head_row
    safe_norm = jnp.where(norm_row > 0, norm_row, 1.0)
    middle = 0.5 * (head_row + norm_row)
    outside = jnp.where(head_own > 0, middle, middle * slack / safe_norm)
    return jnp.where(inside, slack, jnp.where(killed, 0.0, outside))


def body(iterates, residuals, operator, target, cone_id):
    row_count = lax.axis_size("row")
    col_count = lax.axis_size("col")
    row_block = operator.shape[0]
    local_len = iterates.shape[1]
    all_rows = row_block * row_count
    scale_back = math.sqrt(local_len * row_count * col_count / all_rows)
    row_index = lax.axis_index("row")
    row_offset = row_index * row_block
    delta_x = iterates[1:] - iterates[:-1]
    delta_f = residuals[1:] - residuals[:-1]
    last_f = residuals[-1]
    gram_local = jnp.dot(delta_f, delta_f.T, precision=HIGH)
    side_local = jnp.dot(delta_f, last_f, precision=HIGH)
    anchor = iterates[-1] + last_f
    step_dirs = delta_x + delta_f
    gram, right_side = lax.psum((gram_local, side_local), ("row", "col"))
    weights = solve_weights(gram, right_side)
    blended = anchor - jnp.dot(weights, step_dirs, precision=HIGH)
    columns = operator
    partial_value = jnp.zeros((row_block,), jnp.float32) + jnp.dot(
        columns, lax.all_gather(blended, "row", axis=0, tiled=True), precision=HIGH
    )
    image_own = lax.psum(partial_value, "col")
    head_all = jnp.concatenate(
        [jnp.ones((1,), jnp.float32), (cone_id[1:] != cone_id[:-1]).astype(jnp.float32)]
    )
    ids_pad = jnp.concatenate(
        [jnp.full((RIM,), -1, jnp.int32), cone_id, jnp.full((RIM,), -1, jnp.int32)]
    )
    head_pad = jnp.concatenate(
        [jnp.zeros((RIM,), jnp.float32), head_all, jnp.zeros((RIM,), jnp.float32)]
    )
    ids_ext = lax.dynamic_slice_in_dim(ids_pad, row_offset, row_block + 2 * RIM, 0)
    head_ext = lax.dynamic_slice_in_dim(head_pad, row_offset, row_block + 2 * RIM, 0)
    slack_own = lax.dynamic_slice_in_dim(target, row_offset, row_block, 0) - image_own
    slack_ext = with_halo(slack_own, (("row", 0),), RIM)
    slack_own = slack_ext[RIM : RIM + row_block]
    proj_own = window_cones(slack_ext, ids_ext, head_ext, row_block)
    correction = proj_own - slack_own
    columns = operator
    back = lax.psum_scatter(
        jnp.dot(correction, columns, precision=HIGH), "row", scatter_dimension=0, tiled=True
    )
    next_point = blended - scale_back * back
    return (next_point, proj_own)


def solution(mesh):
    return jax.shard_map(
        body,
        mesh=mesh,
        in_specs=(P(None, ("col", "row")), P(None, ("col", "row")), P("row", "col"), P(), P()),
        out_specs=(P(("col", "row")), P("row")),
        check_vma=False,
    )
```

profile of v0, /device:TPU:0, one launch (start us, length us, event | category | flops | bytes accessed | tf_op | source)
XLA Modules:
  0.0 124.1 jit_solution(8513609570144858646)
XLA Ops:
  0.7 1.0 convolution_bitcast_fusion.3
  1.7 1.0 fusion.48
  2.7 42.1 %all-reduce.2 = (f32[10,10]{0,1:T(8,128)S(1)}, f32[10]{0:T(128)S(1)}) all-reduce(f32[10,10]{0,1:T(8,128)S(1)} %fusion.48, f32[10]{0:T(128)S(1)} %convolution_bitcast_fusion.3), channel_id=1, replica_groups=mesh['row'=4,'col'=8] {'row','col'}, use_global_device_ids=true, to_apply=%region_0.0 | all-reduce | flops 110 | bytes 880 | tf_op jit(solution)/shard_map/psum | solution.py:67
  46.1 0.9 cholesky.17
  48.6 0.8 custom-call.10
  49.7 1.4 %fusion.56 = (u32[1]{0:T(128)}, u32[1]{0:T(128)}) fusion(u32[32]{0:T(128)} %constant.89, u32[]{:T(128)S(6)} %add.52, u32[]{:T(128)S(6)} %add.49), kind=kLoop, calls=%fused_computation.136 | loop fusion | bytes 24
  51.7 0.9 fusion
  53.1 9.7 %all-reduce = f32[128]{0:T(128)S(1)} all-reduce(f32[128]{0:T(128)S(1)} %dynamic-update-slice.3), channel_id=1, replica_groups=mesh['row'=4,'col'=8] {'row'}, use_global_device_ids=true, to_apply=%add | all-reduce | flops 128 | bytes 1024
  62.9 1.8 %fusion.43 = f32[1,4096]{1,0:T(1,128)S(1)} fusion(f32[4096,128]{1,0:T(8,128)S(1)} %copy-done, f32[128]{0:T(128)S(1)} %all-reduce), kind=kOutput, calls=%fused_computation.123 | convolution fusion | flops 6291456 | bytes 2114048 | tf_op jit(solution)/shard_map/dot_general | solution.py:71
  64.7 25.9 %psum.23 = f32[4096]{0:T(1024)S(1)} all-reduce(f32[4096]{0:T(1024)S(1)} %bitcast.210), channel_id=1, replica_groups=mesh['row'=4,'col'=8] {'col'}, use_global_device_ids=true, to_apply=%region_5.6 | all-reduce | flops 4096 | bytes 32768 | tf_op jit(solution)/shard_map/psum | solution.py:74
  90.6 0.7 dynamic-slice_subtract_fusion
  91.9 1.3 %collective-permute-start.1 = (f32[16]{0:T(128)}, f32[16]{0:T(128)}, u32[]{:S(2)}, u32[]{:S(2)}) collective-permute-start(f32[16]{0:T(128)} %get-tuple-element.100), channel_id=1, source_target_pairs={{8,0},{16,8},{24,16},{9,1},{17,9},{25,17},{10,2},{18,10},{26,18},{... | collective-permute-start | bytes 200 | tf_op jit(solution)/shard_map/ppermute | solution.py:19
  93.2 5.1 %collective-permute-start = (f32[16]{0:T(128)}, f32[16]{0:T(128)}, u32[]{:S(2)}, u32[]{:S(2)}) collective-permute-start(f32[16]{0:T(128)} %get-tuple-element.101), channel_id=1, source_target_pairs={{0,8},{8,16},{16,24},{1,9},{9,17},{17,25},{2,10},{10,18},{18,26},{... | collective-permute-start | bytes 200 | tf_op jit(solution)/shard_map/ppermute | solution.py:18
  98.6 0.8 fusion.54
  100.8 0.8 stack.351
  101.5 1.6 %stack.319 = s32[31,4096]{1,0:T(8,128)S(1)} concatenate(s32[1,4096]{1,0:T(1,128)} %bitcast.224, s32[1,4096]{1,0:T(1,128)} %bitcast.223, s32[1,4096]{1,0:T(1,128)} %bitcast.222, s32[1,4096]{1,0:T(1,128)} %bitcast.221, s32[1,4096]{1,0:T(1,128)} %bitcast.220, s32[1,4096]{1,0:T(1,128)} %bitcast.219, s32[1,4096]{1,0:T(1,128)} %bitcast.218, s32[1,4096]{1,0:T(1,128)} %bitcast.217, ...), dimensions={0} | concatenate | bytes 1015808 | tf_op jit(solution)/shard_map/stack | solution.py:34
  103.1 1.1 pad_maximum_fusion
  104.2 1.0 fusion.3
  105.2 1.0 fusion.17
  106.2 1.7 %pad_maximum_fusion.1 = (f32[4096]{0:T(1024)S(1)}, f32[4096]{0:T(1024)}, f32[4096]{0:T(1024)}, f32[4096]{0:T(1024)}, f32[4096]{0:T(1024)}, /*index=5*/f32[4096]{...) fusion(f32[4096]{0:T(1024)S(1)} %dynamic-slice_subtract_fusion, f32[16]{0:T(128)} %collective-permute-done), kind=kLoop, calls=%fused_computation.102 | loop fusion | flops 36864 | bytes 163904 | tf_op jit(solution)/shard_map/concatenate | solution.py:20
  108.0 4.1 %stack.383 = f32[31,4096]{1,0:T(8,128)} concatenate(f32[1,4096]{1,0:T(1,128)} %bitcast.202, f32[1,4096]{1,0:T(1,128)} %bitcast.203, f32[1,4096]{1,0:T(1,128)} %bitcast.204, f32[1,4096]{1,0:T(1,128)} %bitcast.205, f32[1,4096]{1,0:T(1,128)} %bitcast.206, f32[1,4096]{1,0:T(1,128)} %bitcast.207, f32[1,4096]{1,0:T(1,128)} %bitcast.208, f32[1,4096]{1,0:T(1,128)} %bitcast.209, ...), dimensions={0} | concatenate | bytes 1015808 | tf_op jit(solution)/shard_map/stack | solution.py:33
  112.1 1.3 %fusion.1 = (f32[4096]{0:T(1024)S(1)}, f32[4096]{0:T(1024)S(1)}) fusion(f32[31,4096]{1,0:T(8,128)} %stack.383, f32[31,4096]{1,0:T(8,128)S(1)} %stack.351, s32[31,4096]{1,0:T(8,128)S(1)} %stack.319, s32[4096]{0:T(1024)S(1)} %get-tuple-element.54), kind=kLoop, calls=%fused_computation.7 | loop fusion | flops 1134592 | bytes 1572864 | tf_op jit(solution)/shard_map/reduce_sum | solution.py:41
  114.0 1.1 convolution_bitcast_fusion.4
  115.1 8.4 %all-reduce.1 = f32[128]{0:T(128)S(1)} all-reduce(f32[128]{0:T(128)S(1)} %convolution_bitcast_fusion.4), channel_id=2, replica_groups=mesh['row'=4,'col'=8] {'row'}, use_global_device_ids=true, to_apply=%region_8.9.clone | all-reduce | flops 128 | bytes 1024
  (34 shorter events, 5.9 us)
Async XLA Ops:
  0.6 62.2 %copy-start = (f32[4096,128]{1,0:T(8,128)S(1)}, f32[4096,128]{1,0:T(8,128)}, u32[]{:S(2)}) copy-start(f32[4096,128]{1,0:T(8,128)} %param.7) | copy-start | bytes 6291460
  0.6 97.7 %copy-start.1 = (s32[16384]{0:T(1024)S(1)}, s32[16384]{0:T(1024)}, u32[]{:S(2)}) copy-start(s32[16384]{0:T(1024)} %param.9) | copy-start | bytes 196612
  52.6 0.5 copy-start.2
  91.9 11.2 %collective-permute-start.1 = (f32[16]{0:T(128)}, f32[16]{0:T(128)}, u32[]{:S(2)}, u32[]{:S(2)}) collective-permute-start(f32[16]{0:T(128)} %get-tuple-element.100), channel_id=1, source_target_pairs={{8,0},{16,8},{24,16},{9,1},{17,9},{25,17},{10,2},{18,10},{26,18},{... | collective-permute-start | bytes 200 | tf_op jit(solution)/shard_map/ppermute | solution.py:19
  93.2 12.0 %collective-permute-start = (f32[16]{0:T(128)}, f32[16]{0:T(128)}, u32[]{:S(2)}, u32[]{:S(2)}) collective-permute-start(f32[16]{0:T(128)} %get-tuple-element.101), channel_id=1, source_target_pairs={{0,8},{8,16},{16,24},{1,9},{9,17},{17,25},{2,10},{10,18},{18,26},{... | collective-permute-start | bytes 200 | tf_op jit(solution)/shard_map/ppermute | solution.py:18
  112.1 11.4 %copy-start.3 = (f32[32]{0:T(128)S(1)}, f32[32]{0:T(128)}, u32[]{:S(2)}) copy-start(f32[32]{0:T(128)} %copy-done.2) | copy-start | bytes 388
where the time goes:
time: 125 us; the launch traced here: 124 us
  blocking collectives  86.1 us (69%)
  other arithmetic  11.8 us (9%)
  local copies, waits for them, and re-layouts  10.9 us (9%)
  starting transfers between devices  6.42 us (5%)
  matrix products  6.11 us (5%)
  between operations  2.75 us (2%)
    psum x1, blocking collectives, body(): gram, right_side = lax.psum((gram_local, side_local), ('row', 'col'))  42.1 us
    psum x1, blocking collectives, body(): image_own = lax.psum(partial_value, 'col')  25.9 us
    unnamed x2, blocking collectives  18.1 us
    ppermute x1, starting transfers between devices, with_halo(): before = lax.ppermute(last, axis, up)  5.14 us
    concatenate x4, other arithmetic, with_halo(): x = jnp.concatenate([before, x, after], axis=dim)  4.81 us
    another operation x1, local copies, waits for them, and re-layouts, window_cones(): slack_win = jnp.stack([slack_ext[RIM + s:RIM + s + length] for s in shifts])  4.14 us
  transfers between devices with their start and end apart: 2, of which 0 were waited for; matrix products, arithmetic and copies ran while one was open for 5% of the time, Pallas kernels for 0%

commit v1 on v0

--- a/solution.py
+++ b/solution.py
@@ -71,7 +71,11 @@
     partial_value = jnp.zeros((row_block,), jnp.float32) + jnp.dot(
         columns, lax.all_gather(blended, "row", axis=0, tiled=True), precision=HIGH
     )
-    image_own = lax.psum(partial_value, "col")
+    image_own = partial_value
+    for hop in (1, 2, 4):
+        image_own = image_own + lax.ppermute(
+            image_own, "col", [(dev, dev ^ hop) for dev in range(8)]
+        )
     head_all = jnp.concatenate(
         [jnp.ones((1,), jnp.float32), (cone_id[1:] != cone_id[:-1]).astype(jnp.float32)]
     )

time: 125 us -> 104 us (0.83)
  blocking collectives: 86.1 us -> 62.4 us
  starting transfers between devices: 6.42 us -> 9.7 us
  other arithmetic: 11.8 us -> 8.68 us
  waiting for transfers between devices: 0.01 us -> 2.83 us
    psum x1 -> x0, blocking collectives: 25.9 us -> none  [body(): image_own = lax.psum(partial_value, 'col')]
    ppermute x0 -> x3, starting transfers between devices: none -> 3.87 us  [body(): lax.ppermute(image_own, 'col', [(dev, dev ^ hop) for dev in range(8)])]
    concatenate x4, other arithmetic: 4.81 us -> 1.04 us  [with_halo(): x = jnp.concatenate([before, x, after], axis=dim)]
    unnamed x2, blocking collectives: 18.1 us -> 20.3 us
    ppermute x0 -> x3, waiting for transfers between devices: none -> 1.77 us  [body(): lax.ppermute(image_own, 'col', [(dev, dev ^ hop) for dev in range(8)])]
  transfers between devices with their start and end apart: 2 -> 5, of which waited for: 0 -> 3; matrix products, arithmetic and copies ran while one was open for 5% -> 4% of each run, Pallas kernels for 0% -> 0%
where the time goes in v1:
time: 104 us; the launch traced here: 103 us
  blocking collectives  62.4 us (60%)
  local copies, waits for them, and re-layouts  10.5 us (10%)
  starting transfers between devices  9.7 us (9%)
  other arithmetic  8.68 us (8%)
  matrix products  6.11 us (6%)
  waiting for transfers between devices  2.83 us (3%)
  between operations  2.7 us (3%)
    psum x1, blocking collectives, body(): gram, right_side = lax.psum((gram_local, side_local), ('row', 'col'))  42.1 us
    unnamed x2, blocking collectives  20.3 us
    ppermute x1, starting transfers between devices, with_halo(): before = lax.ppermute(last, axis, up)  4.55 us
    another operation x1, local copies, waits for them, and re-layouts, window_cones(): slack_win = jnp.stack([slack_ext[RIM + s:RIM + s + length] for s in shifts])  4.14 us
    ppermute x3, starting transfers between devices, body(): lax.ppermute(image_own, 'col', [(dev, dev ^ hop) for dev in range(8)])  3.87 us
  transfers between devices with their start and end apart: 5, of which 3 were waited for; matrix products, arithmetic and copies ran while one was open for 4% of the time, Pallas kernels for 0%

profile of v1, /device:TPU:0, one launch (start us, length us, event | category | flops | bytes accessed | tf_op | source)
XLA Modules:
  0.0 103.0 jit_solution(9117856282770932098)
XLA Ops:
  0.7 1.0 convolution_bitcast_fusion.3
  1.7 1.0 fusion.48
  2.7 42.1 %all-reduce.2 = (f32[10,10]{0,1:T(8,128)S(1)}, f32[10]{0:T(128)S(1)}) all-reduce(f32[10,10]{0,1:T(8,128)S(1)} %fusion.48, f32[10]{0:T(128)S(1)} %convolution_bitcast_fusion.3), channel_id=1, replica_groups=mesh['row'=4,'col'=8] {'row','col'}, use_global_device_ids=true, to_apply=%region_0.0 | all-reduce | flops 110 | bytes 880 | tf_op jit(solution)/shard_map/psum | solution.py:67
  46.1 0.9 cholesky.17
  48.6 0.8 custom-call.10
  49.7 1.3 %fusion.56 = (u32[1]{0:T(128)}, u32[1]{0:T(128)}) fusion(u32[32]{0:T(128)} %constant.89, u32[]{:T(128)S(6)} %add.62, u32[]{:T(128)S(6)} %add.59), kind=kLoop, calls=%fused_computation.136 | loop fusion | bytes 24
  51.7 0.9 fusion
  53.3 9.7 %all-reduce = f32[128]{0:T(128)S(1)} all-reduce(f32[128]{0:T(128)S(1)} %dynamic-update-slice.3), channel_id=1, replica_groups=mesh['row'=4,'col'=8] {'row'}, use_global_device_ids=true, to_apply=%add | all-reduce | flops 128 | bytes 1024
  63.0 1.8 %fusion.43 = f32[1,4096]{1,0:T(1,128)S(1)} fusion(f32[4096,128]{1,0:T(8,128)S(1)} %copy-done, f32[128]{0:T(128)S(1)} %all-reduce), kind=kOutput, calls=%fused_computation.123 | convolution fusion | flops 6291456 | bytes 2114048 | tf_op jit(solution)/shard_map/dot_general | solution.py:71
  66.1 1.5 %collective-permute-start.1 = (f32[4096]{0:T(1024)S(1)}, f32[4096]{0:T(1024)S(1)}, u32[]{:S(2)}, u32[]{:S(2)}) collective-permute-start(f32[4096]{0:T(1024)S(1)} %add.55), channel_id=1, source_target_pairs={{0,2},{1,3},{2,0},{3,1},{4,6},{5,7},{6,4},{7,5},{8,10},{9,11},{10,... | collective-permute-start | bytes 49160 | tf_op jit(solution)/shard_map/ppermute | solution.py:76
  67.6 0.8 fusion.54
  68.3 1.5 %collective-permute-done.1 = f32[4096]{0:T(1024)S(1)} collective-permute-done((f32[4096]{0:T(1024)S(1)}, f32[4096]{0:T(1024)S(1)}, u32[]{:S(2)}, u32[]{:S(2)}) %collective-permute-start.1) | collective-permute-done | bytes 16416 | tf_op jit(solution)/shard_map/ppermute | solution.py:76
  70.4 2.3 %collective-permute-start.2 = (f32[4096]{0:T(1024)}, f32[4096]{0:T(1024)}, u32[]{:S(2)}, u32[]{:S(2)}) collective-permute-start(f32[4096]{0:T(1024)} %add.56), channel_id=1, source_target_pairs={{0,4},{1,5},{2,6},{3,7},{4,0},{5,1},{6,2},{7,3},{8,12},{9,13},{10,... | collective-permute-start | bytes 49160 | tf_op jit(solution)/shard_map/ppermute | solution.py:76
  73.5 0.8 stack.351
  74.2 1.6 %stack.319 = s32[31,4096]{1,0:T(8,128)S(1)} concatenate(s32[1,4096]{1,0:T(1,128)} %bitcast.225, s32[1,4096]{1,0:T(1,128)} %bitcast.224, s32[1,4096]{1,0:T(1,128)} %bitcast.223, s32[1,4096]{1,0:T(1,128)} %bitcast.222, s32[1,4096]{1,0:T(1,128)} %bitcast.221, s32[1,4096]{1,0:T(1,128)} %bitcast.220, s32[1,4096]{1,0:T(1,128)} %bitcast.219, s32[1,4096]{1,0:T(1,128)S(1)} %bitcast.218, ...), dimensions={0} | concatenate | bytes 1015808 | tf_op jit(solution)/shard_map/stack | solution.py:34
  75.8 0.8 add_subtract_fusion
  76.6 1.3 %collective-permute-start.4 = (f32[16]{0:T(128)S(1)}, f32[16]{0:T(128)S(1)}, u32[]{:S(2)}, u32[]{:S(2)}) collective-permute-start(f32[16]{0:T(128)S(1)} %get-tuple-element.100), channel_id=1, source_target_pairs={{8,0},{16,8},{24,16},{9,1},{17,9},{25,17},{10,2},{18,10},{26,18},{... | collective-permute-start | bytes 200 | tf_op jit(solution)/shard_map/ppermute | solution.py:19
  77.9 4.5 %collective-permute-start.3 = (f32[16]{0:T(128)S(1)}, f32[16]{0:T(128)S(1)}, u32[]{:S(2)}, u32[]{:S(2)}) collective-permute-start(f32[16]{0:T(128)S(1)} %get-tuple-element.101), channel_id=1, source_target_pairs={{0,8},{8,16},{16,24},{1,9},{9,17},{17,25},{2,10},{10,18},{18,26},{... | collective-permute-start | bytes 200 | tf_op jit(solution)/shard_map/ppermute | solution.py:18
  82.7 1.0 %collective-permute-done.3 = f32[16]{0:T(128)S(1)} collective-permute-done((f32[16]{0:T(128)S(1)}, f32[16]{0:T(128)S(1)}, u32[]{:S(2)}, u32[]{:S(2)}) %collective-permute-start.3) | collective-permute-done | bytes 96 | tf_op jit(solution)/shard_map/ppermute | solution.py:18
  83.9 0.7 pad_maximum_fusion.1
  84.6 4.1 %stack.383 = f32[31,4096]{1,0:T(8,128)} concatenate(f32[1,4096]{1,0:T(1,128)} %bitcast.204, f32[1,4096]{1,0:T(1,128)} %bitcast.205, f32[1,4096]{1,0:T(1,128)} %bitcast.206, f32[1,4096]{1,0:T(1,128)} %bitcast.207, f32[1,4096]{1,0:T(1,128)} %bitcast.208, f32[1,4096]{1,0:T(1,128)} %bitcast.209, f32[1,4096]{1,0:T(1,128)} %bitcast.210, f32[1,4096]{1,0:T(1,128)} %bitcast.211, ...), dimensions={0} | concatenate | bytes 1015808 | tf_op jit(solution)/shard_map/stack | solution.py:33
  88.7 1.3 %fusion.1 = (f32[4096]{0:T(1024)S(1)}, f32[4096]{0:T(1024)S(1)}) fusion(f32[31,4096]{1,0:T(8,128)} %stack.383, f32[31,4096]{1,0:T(8,128)S(1)} %stack.351, s32[31,4096]{1,0:T(8,128)S(1)} %stack.319, s32[4096]{0:T(1024)S(1)} %get-tuple-element.54), kind=kLoop, calls=%fused_computation.7 | loop fusion | flops 1134592 | bytes 1572864 | tf_op jit(solution)/shard_map/reduce_sum | solution.py:41
  90.6 1.1 %convolution_bitcast_fusion.4 = f32[128]{0:T(128)S(1)} fusion(f32[4096,1]{0,1:T(1,128)S(1)} %bitcast.212, f32[4096,128]{1,0:T(8,128)S(1)} %copy-done), kind=kOutput, calls=%fused_computation.5 | convolution fusion | flops 6291456 | bytes 2114048 | tf_op jit(solution)/shard_map/dot_general | solution.py:97
  91.8 10.6 %all-reduce.1 = f32[128]{0:T(128)S(1)} all-reduce(f32[128]{0:T(128)S(1)} %convolution_bitcast_fusion.4), channel_id=2, replica_groups=mesh['row'=4,'col'=8] {'row'}, use_global_device_ids=true, to_apply=%region_7.8.clone | all-reduce | flops 128 | bytes 1024
  (41 shorter events, 6.9 us)
Async XLA Ops:
  0.6 62.4 %copy-start = (f32[4096,128]{1,0:T(8,128)S(1)}, f32[4096,128]{1,0:T(8,128)}, u32[]{:S(2)}) copy-start(f32[4096,128]{1,0:T(8,128)} %param.7) | copy-start | bytes 6291460
  0.6 64.2 %copy-start.1 = (s32[16384]{0:T(1024)S(1)}, s32[16384]{0:T(1024)}, u32[]{:S(2)}) copy-start(s32[16384]{0:T(1024)} %param.9) | copy-start | bytes 196612
  52.6 0.5 copy-start.2
  64.8 1.2 %collective-permute-start = (f32[4096]{0:T(1024)S(1)}, f32[4096]{0:T(1024)S(1)}, u32[]{:S(2)}, u32[]{:S(2)}) collective-permute-start(f32[4096]{0:T(1024)S(1)} %bitcast.180), channel_id=1, source_target_pairs={{0,1},{1,0},{2,3},{3,2},{4,5},{5,4},{6,7},{7,6},{8,9},{9,8},{10,11... | collective-permute-start | bytes 49160 | tf_op jit(solution)/shard_map/ppermute | solution.py:76
  66.1 3.7 %collective-permute-start.1 = (f32[4096]{0:T(1024)S(1)}, f32[4096]{0:T(1024)S(1)}, u32[]{:S(2)}, u32[]{:S(2)}) collective-permute-start(f32[4096]{0:T(1024)S(1)} %add.55), channel_id=1, source_target_pairs={{0,2},{1,3},{2,0},{3,1},{4,6},{5,7},{6,4},{7,5},{8,10},{9,11},{10,... | collective-permute-start | bytes 49160 | tf_op jit(solution)/shard_map/ppermute | solution.py:76
  70.4 5.4 %collective-permute-start.2 = (f32[4096]{0:T(1024)}, f32[4096]{0:T(1024)}, u32[]{:S(2)}, u32[]{:S(2)}) collective-permute-start(f32[4096]{0:T(1024)} %add.56), channel_id=1, source_target_pairs={{0,4},{1,5},{2,6},{3,7},{4,0},{5,1},{6,2},{7,3},{8,12},{9,13},{10,... | collective-permute-start | bytes 49160 | tf_op jit(solution)/shard_map/ppermute | solution.py:76
  76.6 5.8 %collective-permute-start.4 = (f32[16]{0:T(128)S(1)}, f32[16]{0:T(128)S(1)}, u32[]{:S(2)}, u32[]{:S(2)}) collective-permute-start(f32[16]{0:T(128)S(1)} %get-tuple-element.100), channel_id=1, source_target_pairs={{8,0},{16,8},{24,16},{9,1},{17,9},{25,17},{10,2},{18,10},{26,18},{... | collective-permute-start | bytes 200 | tf_op jit(solution)/shard_map/ppermute | solution.py:19
  77.9 5.8 %collective-permute-start.3 = (f32[16]{0:T(128)S(1)}, f32[16]{0:T(128)S(1)}, u32[]{:S(2)}, u32[]{:S(2)}) collective-permute-start(f32[16]{0:T(128)S(1)} %get-tuple-element.101), channel_id=1, source_target_pairs={{0,8},{8,16},{16,24},{1,9},{9,17},{17,25},{2,10},{10,18},{18,26},{... | collective-permute-start | bytes 200 | tf_op jit(solution)/shard_map/ppermute | solution.py:18
  88.7 13.6 %copy-start.3 = (f32[32]{0:T(128)S(1)}, f32[32]{0:T(128)}, u32[]{:S(2)}) copy-start(f32[32]{0:T(128)} %copy-done.2) | copy-start | bytes 388
